TPU v7x, 32 devices: a whole 2x2x4 slice. The times are simulated.
32 devices in a mesh: lat: 4 (over z), lon: 8 (over y, x, core).
Axes of the slice: x: 2, y: 2, z: 4, core: 2. Of those that a mesh axis runs over, the one named last changes fastest.
Arguments:
- grid_latent: bfloat16 [16384, 512], P(('lat', 'lon')), may hold values from -6 to 6
- mesh_latent: bfloat16 [4096, 512], P(('lat', 'lon')), may hold values from -6 to 6
- block_weights: bfloat16 [4, 3, 512, 512], replicated, may hold values from -0.25 to 0.25
- block_gains: float32 [4, 512], replicated, may hold values from 0.5 to 1.5
- grid_cot: bfloat16 [16384, 512], P(('lat', 'lon')), may hold values from -0.046875 to 0.046875
- encode_rows: int32 [32, 32, 4], P(('lat', 'lon')), may hold values from 0 to 511
- encode_senders: int32 [32, 1536], P(('lat', 'lon')), may hold values from 0 to 127, as said below
- encode_receivers: int32 [32, 1536], P(('lat', 'lon')), may hold values from 0 to 127, as said below
- encode_blocks: int32 [32], P(('lat', 'lon')), may hold values from 4 to 12, as said below
- process_rows: int32 [32, 32, 4], P(('lat', 'lon')), may hold values from 0 to 127
- process_senders: int32 [32, 1536], P(('lat', 'lon')), may hold values from 0 to 127, as said below
- process_receivers: int32 [32, 1536], P(('lat', 'lon')), may hold values from 0 to 127, as said below
- process_blocks: int32 [32], P(('lat', 'lon')), may hold values from 4 to 12, as said below
- decode_rows: int32 [32, 32, 4], P(('lat', 'lon')), may hold values from 0 to 127
- decode_senders: int32 [32, 1536], P(('lat', 'lon')), may hold values from 0 to 127, as said below
- decode_receivers: int32 [32, 1536], P(('lat', 'lon')), may hold values from 0 to 511, as said below
- decode_blocks: int32 [32], P(('lat', 'lon')), may hold values from 4 to 12, as said below
Outputs:
- grid_out: bfloat16 [16384, 512], P(('lat', 'lon'))
- weight_grad: bfloat16 [4, 3, 512, 512], replicated
- gain_grad: float32 [4, 512], replicated
Inputs may be any that keep to these rules, and one draw needn't show every extreme that they name: `encode_senders`: on every device each of the 128 received slots is named by some edge of the first 4 blocks. `encode_receivers`: on every device each of its 128 mesh rows is named by some edge of the first 4 blocks. `encode_blocks`: some device has 12 live blocks. `process_senders`: on every device each of the 128 received slots is named by some edge of the first 4 blocks. `process_receivers`: on every device each of its 128 mesh rows is named by some edge of the first 4 blocks. `process_blocks`: some device has 12 live blocks. `decode_senders`: on every device each of the 128 received slots is named by some edge of the first 4 blocks. `decode_receivers`: on every device each of its 512 grid rows is named by some edge of the first 4 blocks. `decode_blocks`: some device has 12 live blocks.
All inputs are finite; a program needn't handle non-finite values.
Results may differ from a plain program's by a relative error of at most 0.017.
Values may be sent and summed in bfloat16 or wider, within the bound.
No kernel may reach another device: no remote copies, remote signals or barrier semaphores. Data moves between devices by JAX's collectives and lax.ppermute only.
A program may use at most 128 MiB of HBM per device.

v0:
```python
import jax
import jax.numpy as jnp
from jax import lax
from jax.sharding import PartitionSpec as P

LAYERS = 2
EDGE_BLOCK = 128
EPSILON = 1e-05


def silu_slope(values):
    sigma = jax.nn.sigmoid(values)
    return sigma * (1.0 + values * (1.0 - sigma))


def transposed_product(left, right):
    return lax.dot_general(
        left, right, (((0,), (0,)), ((), ())), preferred_element_type=jnp.float32
    )


def back_product(grad, weight):
    return lax.dot_general(
        grad, weight, (((1,), (1,)), ((), ())), preferred_element_type=jnp.float32
    )


def projected(latent, weight):
    return jnp.dot(latent, weight, preferred_element_type=jnp.float32).astype(jnp.bfloat16)


def edge_forward(
    slot_vals, proj_recv, latent_recv, senders, receivers, live_mask, weight_out, block_gain
):
    preact = slot_vals[senders].astype(jnp.float32) + proj_recv[receivers].astype(jnp.float32)
    hidden = jax.nn.silu(preact) * live_mask[:, None]
    summed = jax.ops.segment_sum(hidden, receivers, num_segments=proj_recv.shape[0]).astype(
        jnp.bfloat16
    )
    mixed = jnp.dot(summed, weight_out, preferred_element_type=jnp.float32)
    centred = mixed - jnp.mean(mixed, axis=-1, keepdims=True)
    inv_scale = lax.rsqrt(jnp.mean(centred * centred, axis=-1, keepdims=True) + EPSILON)
    normed = centred * inv_scale
    output = (latent_recv.astype(jnp.float32) + normed * block_gain).astype(jnp.bfloat16)
    return (output, preact, summed, normed, inv_scale)


def edge_backward(
    grad_out,
    preact,
    summed,
    normed,
    inv_scale,
    senders,
    receivers,
    live_mask,
    weight_out,
    block_gain,
    recv_count,
    slot_count,
):
    gain_part = jnp.sum(grad_out * normed, axis=0)
    grad_normed = grad_out * block_gain
    grad_mixed = inv_scale * (
        grad_normed
        - jnp.mean(grad_normed, axis=-1, keepdims=True)
        - normed * jnp.mean(grad_normed * normed, axis=-1, keepdims=True)
    )
    grad_mixed = grad_mixed.astype(jnp.bfloat16)
    out_part = transposed_product(summed, grad_mixed)
    grad_summed = back_product(grad_mixed, weight_out)
    grad_pre = grad_summed[receivers] * live_mask[:, None] * silu_slope(preact)
    grad_recv = jax.ops.segment_sum(grad_pre, receivers, num_segments=recv_count).astype(
        jnp.bfloat16
    )
    grad_slots = jax.ops.segment_sum(grad_pre, senders, num_segments=slot_count).astype(
        jnp.bfloat16
    )
    return (grad_recv, grad_slots, out_part, gain_part)


def trade(buffer):
    return lax.all_to_all(buffer, ("lat", "lon"), split_axis=0, concat_axis=0, tiled=True)


def graph_parts(send_rows, senders, receivers, block_count):
    positions = jnp.arange(senders.shape[1], dtype=jnp.int32) // EDGE_BLOCK
    live_mask = (positions < block_count[0]).astype(jnp.float32)
    return (send_rows[0], senders[0], receivers[0], live_mask)


def run_forward(latent_send, latent_recv, weights, block_gain, graph):
    send_rows, senders, receivers, live_mask = graph
    proj_send = projected(latent_send, weights[0])
    outgoing = proj_send[send_rows]
    proj_recv = projected(latent_recv, weights[1])
    slot_vals = trade(outgoing).reshape(-1, proj_send.shape[1])
    output, preact, summed, normed, inv_scale = edge_forward(
        slot_vals, proj_recv, latent_recv, senders, receivers, live_mask, weights[2], block_gain
    )
    return (output, (preact, summed, normed, inv_scale, slot_vals.shape[0]))


def run_backward(grad_out, latent_send, latent_recv, weights, block_gain, graph, saved):
    send_rows, senders, receivers, live_mask = graph
    preact, summed, normed, inv_scale, slot_count = saved
    grad_recv, grad_slots, out_part, gain_part = edge_backward(
        grad_out,
        preact,
        summed,
        normed,
        inv_scale,
        senders,
        receivers,
        live_mask,
        weights[2],
        block_gain,
        latent_recv.shape[0],
        slot_count,
    )
    width = grad_slots.shape[1]
    returned = trade(grad_slots.reshape(send_rows.shape + (width,)))
    grad_send = (
        jnp.zeros((latent_send.shape[0], width), jnp.float32)
        .at[send_rows.reshape(-1)]
        .add(returned.reshape(-1, width).astype(jnp.float32))
        .astype(jnp.bfloat16)
    )
    grad_weights = jnp.stack(
        [
            transposed_product(latent_send, grad_send),
            transposed_product(latent_recv, grad_recv),
            out_part,
        ]
    )
    return (grad_weights, gain_part, grad_send, grad_recv)


def settle(grad_weights, gain_part):
    return (grad_weights, gain_part)


def shards(
    grid_latent,
    mesh_latent,
    block_weights,
    block_gains,
    grid_cot,
    encode_rows,
    encode_senders,
    encode_receivers,
    encode_blocks,
    process_rows,
    process_senders,
    process_receivers,
    process_blocks,
    decode_rows,
    decode_senders,
    decode_receivers,
    decode_blocks,
):
    encode = graph_parts(encode_rows, encode_senders, encode_receivers, encode_blocks)
    process = graph_parts(process_rows, process_senders, process_receivers, process_blocks)
    decode = graph_parts(decode_rows, decode_senders, decode_receivers, decode_blocks)
    latents = [mesh_latent]
    saves = []
    output, saved = run_forward(grid_latent, mesh_latent, block_weights[0], block_gains[0], encode)
    latents.append(output)
    saves.append(saved)
    for layer_id in range(LAYERS):
        current = latents[-1]
        output, saved = run_forward(
            current, current, block_weights[layer_id + 1], block_gains[layer_id + 1], process
        )
        latents.append(output)
        saves.append(saved)
    last_id = LAYERS + 1
    grid_out, decode_saved = run_forward(
        latents[-1], grid_latent, block_weights[last_id], block_gains[last_id], decode
    )
    weight_parts = [None] * (LAYERS + 2)
    gain_parts = [None] * (LAYERS + 2)
    grad_weights, gain_part, grad_send, grad_recv = run_backward(
        grid_cot.astype(jnp.float32),
        latents[-1],
        grid_latent,
        block_weights[last_id],
        block_gains[last_id],
        decode,
        decode_saved,
    )
    weight_parts[last_id], gain_parts[last_id] = settle(grad_weights, gain_part)
    grad_mesh = back_product(grad_send, block_weights[last_id][0])
    for layer_id in reversed(range(LAYERS)):
        block_id = layer_id + 1
        current = latents[block_id]
        grad_weights, gain_part, grad_send, grad_recv = run_backward(
            grad_mesh,
            current,
            current,
            block_weights[block_id],
            block_gains[block_id],
            process,
            saves[block_id],
        )
        weight_parts[block_id], gain_parts[block_id] = settle(grad_weights, gain_part)
        grad_mesh = (
            grad_mesh
            + back_product(grad_recv, block_weights[block_id][1])
            + back_product(grad_send, block_weights[block_id][0])
        )
    grad_weights, gain_part, grad_send, grad_recv = run_backward(
        grad_mesh, grid_latent, mesh_latent, block_weights[0], block_gains[0], encode, saves[0]
    )
    weight_parts[0], gain_parts[0] = settle(grad_weights, gain_part)
    weight_stack = jnp.stack(weight_parts)
    gain_stack = jnp.stack(gain_parts)
    weight_stack, gain_stack = lax.psum((weight_stack, gain_stack), ("lat", "lon"))
    return (grid_out, weight_stack.astype(jnp.bfloat16), gain_stack)


def solution(mesh):
    return jax.shard_map(
        shards,
        mesh=mesh,
        in_specs=(
            P(("lat", "lon"), None),
            P(("lat", "lon"), None),
            P(),
            P(),
            P(("lat", "lon"), None),
            P(("lat", "lon"), None, None),
            P(("lat", "lon"), None),
            P(("lat", "lon"), None),
            P(("lat", "lon")),
            P(("lat", "lon"), None, None),
            P(("lat", "lon"), None),
            P(("lat", "lon"), None),
            P(("lat", "lon")),
            P(("lat", "lon"), None, None),
            P(("lat", "lon"), None),
            P(("lat", "lon"), None),
            P(("lat", "lon")),
        ),
        out_specs=(P(("lat", "lon"), None), P(), P()),
        check_vma=False,
    )
```

profile of v0, /device:TPU:0, one launch (start us, length us, event | category | flops | bytes accessed | tf_op | source)
XLA Modules:
  0.0 602.4 jit_solution(12311952505016923633)
XLA Ops:
  4.9 7.3 %all-to-all-start = ((bf16[32,4,512]{2,1,0:T(4,128)(2,1)}), bf16[32,4,512]{2,1,0:T(4,128)(2,1)S(1)}, u32[]{:S(2)}, u32[]{:S(2)}) async-start(bf16[32,4,512]{2,1,0:T(4,128)(2,1)} %reshape.518), calls=%async_computation | async-start | bytes 262144 | tf_op jit(solution)/shard_map/all_to_all | solution.py:83
  25.8 5.4 gather_fusion.1
  31.2 11.8 %scatter_custom_fusion = f32[128,512]{1,0:T(8,128)S(1)} fusion(s32[1536]{0:T(1024)S(1)} %reduce.1, bf16[1536,512]{1,0:T(8,128)(2,1)S(1)} %gather_fusion.2, bf16[1536,512]{1,0:T(8,128)(2,1)} %gather_fusion.1, f32[1536]{0:T(1024)S(1)} %fusion.133, f32[]{:T(128)} %constant.63.clone.1, f32[]{:T(128)} %constant.59.clone.1), kind=kCustom, calls=%fused_computation.56 | custom fusion | flops 7077888 | bytes 3416072 | tf_op jit(solution)/shard_map/scatter-add | solution.py:37
  48.3 5.8 all-to-all-start.1
  56.2 5.4 gather_fusion.5
  62.3 5.4 gather_fusion.4
  67.8 11.9 %scatter_custom_fusion.1 = f32[128,512]{1,0:T(8,128)S(1)} fusion(s32[1536]{0:T(1024)S(1)} %reduce.4, bf16[1536,512]{1,0:T(8,128)(2,1)} %gather_fusion.5, bf16[1536,512]{1,0:T(8,128)(2,1)} %gather_fusion.4, f32[1536]{0:T(1024)S(1)} %fusion.134, f32[]{:T(128)} %constant.63.clone.1, f32[]{:T(128)} %constant.59.clone.1), kind=kCustom, calls=%fused_computation.51 | custom fusion | flops 7077888 | bytes 3416072 | tf_op jit(solution)/shard_map/scatter-add | solution.py:37
  85.0 5.2 all-to-all-start.2
  92.0 5.4 gather_fusion.8
  98.4 5.4 gather_fusion.7
  103.8 11.7 %scatter_custom_fusion.2 = f32[128,512]{1,0:T(8,128)S(1)} fusion(s32[1536]{0:T(1024)S(1)} %reduce.4, bf16[1536,512]{1,0:T(8,128)(2,1)} %gather_fusion.8, bf16[1536,512]{1,0:T(8,128)(2,1)} %gather_fusion.7, f32[1536]{0:T(1024)S(1)} %fusion.134, f32[]{:T(128)} %constant.63.clone.1, f32[]{:T(128)} %constant.59.clone.1), kind=kCustom, calls=%fused_computation.46 | custom fusion | flops 7077888 | bytes 3416072 | tf_op jit(solution)/shard_map/scatter-add | solution.py:37
  121.4 4.9 all-to-all-start.3
  136.2 5.4 gather_fusion.11
  142.3 5.7 gather_fusion.10
  148.0 13.0 %scatter_custom_fusion.3 = f32[512,512]{1,0:T(8,128)} fusion(s32[1536]{0:T(1024)} %reduce, bf16[1536,512]{1,0:T(8,128)(2,1)S(1)} %copy-done.3, bf16[1536,512]{1,0:T(8,128)(2,1)} %gather_fusion.10, f32[1536]{0:T(1024)} %fusion.135, f32[]{:T(128)} %constant.63.clone.1, f32[]{:T(128)} %constant.59.clone.1), kind=kCustom, calls=%fused_computation.41 | custom fusion | flops 7077888 | bytes 4203520 | tf_op jit(solution)/shard_map/scatter-add | solution.py:37
  167.2 4.9 gather_fusion.12
  177.0 11.0 %scatter_custom_fusion.4 = f32[128,512]{1,0:T(8,128)} fusion(s32[1536]{0:T(1024)} %reduce.10, f32[1536,512]{1,0:T(8,128)} %multiply_multiply_fusion.3, f32[]{:T(128)} %constant.59.clone.1), kind=kCustom, calls=%fused_computation.206 | custom fusion | flops 786432 | bytes 262656 | tf_op jit(solution)/shard_map/scatter-add | solution.py:76
  189.7 5.8 all-to-all-start.4
  198.1 10.5 %scatter_custom_fusion.15 = f32[512,512]{1,0:T(8,128)S(1)} fusion(s32[1536]{0:T(1024)} %reduce, f32[1536,512]{1,0:T(8,128)} %multiply_multiply_fusion.3, f32[]{:T(128)} %constant.59.clone.1), kind=kCustom, calls=%fused_computation.141 | custom fusion | flops 786432 | bytes 1049088 | tf_op jit(solution)/shard_map/scatter-add | solution.py:73
  220.9 4.9 gather_fusion.13
  230.3 10.4 %scatter_custom_fusion.6 = f32[128,512]{1,0:T(8,128)S(1)} fusion(s32[1536]{0:T(1024)} %copy-done.68, f32[1536,512]{1,0:T(8,128)} %multiply_multiply_fusion.2, f32[]{:T(128)} %constant.59.clone.1), kind=kCustom, calls=%fused_computation.202 | custom fusion | flops 786432 | bytes 262656 | tf_op jit(solution)/shard_map/scatter-add | solution.py:73
  240.7 10.3 %scatter_custom_fusion.7 = f32[128,512]{1,0:T(8,128)S(1)} fusion(s32[1536]{0:T(1024)} %reduce.11, f32[1536,512]{1,0:T(8,128)} %multiply_multiply_fusion.2, f32[]{:T(128)} %constant.59.clone.1), kind=kCustom, calls=%fused_computation.200 | custom fusion | flops 786432 | bytes 262656 | tf_op jit(solution)/shard_map/scatter-add | solution.py:76
  251.7 6.0 all-to-all-start.5
  274.9 4.9 gather_fusion.14
  284.4 10.4 %scatter_custom_fusion.9 = f32[128,512]{1,0:T(8,128)S(1)} fusion(s32[1536]{0:T(1024)} %copy-done.68, f32[1536,512]{1,0:T(8,128)} %multiply_multiply_fusion.1, f32[]{:T(128)} %constant.59.clone.1), kind=kCustom, calls=%fused_computation.196 | custom fusion | flops 786432 | bytes 262656 | tf_op jit(solution)/shard_map/scatter-add | solution.py:73
  294.8 10.3 %scatter_custom_fusion.10 = f32[128,512]{1,0:T(8,128)S(1)} fusion(s32[1536]{0:T(1024)} %reduce.11, f32[1536,512]{1,0:T(8,128)} %multiply_multiply_fusion.1, f32[]{:T(128)} %constant.59.clone.1), kind=kCustom, calls=%fused_computation.194 | custom fusion | flops 786432 | bytes 262656 | tf_op jit(solution)/shard_map/scatter-add | solution.py:76
  327.1 4.9 gather_fusion.15
  336.4 10.5 %scatter_custom_fusion.14 = f32[128,512]{1,0:T(8,128)S(1)} fusion(s32[1536]{0:T(1024)} %copy-done.67, f32[1536,512]{1,0:T(8,128)} %multiply_multiply_fusion, f32[]{:T(128)} %constant.59.clone.1), kind=kCustom, calls=%fused_computation.188 | custom fusion | flops 786432 | bytes 262656 | tf_op jit(solution)/shard_map/scatter-add | solution.py:73
  346.9 10.3 %scatter_custom_fusion.12 = f32[128,512]{1,0:T(8,128)S(1)} fusion(s32[1536]{0:T(1024)} %reduce.9, f32[1536,512]{1,0:T(8,128)} %multiply_multiply_fusion, f32[]{:T(128)} %constant.59.clone.1), kind=kCustom, calls=%fused_computation.190 | custom fusion | flops 786432 | bytes 262656 | tf_op jit(solution)/shard_map/scatter-add | solution.py:76
  375.9 6.6 %pad_maximum_fusion = f32[4,3,512,512]{2,3,1,0:T(8,128)} fusion(f32[1,3,512,512]{2,3,1,0:T(8,128)S(1)} %copy-done.4, f32[1,3,512,512]{2,3,1,0:T(8,128)S(1)} %copy-done.5, f32[1,3,512,512]{2,3,1,0:T(8,128)} %maximum_bitcast_fusion.1, f32[1,3,512,512]{2,3,1,0:T(8,128)S(1)} %maximum_bitcast_fusion), kind=kLoop, calls=%fused_computation.32 | loop fusion | flops 9437184 | bytes 25165824 | tf_op jit(solution)/shard_map/stack | solution.py:216
  382.5 210.8 %all-reduce.2 = (bf16[4,3,512,512]{2,3,1,0:T(8,128)(2,1)}, f32[4,512]{1,0:T(4,128)}) all-reduce(f32[4,3,512,512]{2,3,1,0:T(8,128)} %pad_maximum_fusion, f32[4,512]{1,0:T(4,128)S(1)} %pad_maximum_fusion.1), channel_id=1, replica_groups=mesh['lat'=4,'lon'=8] {'lat','lon'}, use_global_device_ids=true, to_apply=%region_32.33 | all-reduce | flops 3147776 | bytes 18890752 | tf_op jit(solution)/shard_map/psum | solution.py:218
  593.3 8.6 %copy.57 = bf16[4,3,512,512]{3,2,1,0:T(8,128)(2,1)} copy(bf16[4,3,512,512]{2,3,1,0:T(8,128)(2,1)} %get-tuple-element.21) | data formatting | bytes 12582912
  (310 shorter events, 147.0 us)
Async XLA Ops:
  0.7 15.2 %copy-start.66 = (f32[4,512]{1,0:T(4,128)S(1)}, f32[4,512]{1,0:T(4,128)}, u32[]{:S(2)}) copy-start(f32[4,512]{1,0:T(4,128)} %param.20) | copy-start | bytes 24580
  0.7 17.4 %copy-start.37 = (bf16[128,512]{1,0:T(8,128)(2,1)S(1)}, bf16[128,512]{1,0:T(8,128)(2,1)}, u32[]{:S(2)}) copy-start(bf16[128,512]{1,0:T(8,128)(2,1)} %param.18) | copy-start | bytes 393220
  4.9 20.8 %all-to-all-start = ((bf16[32,4,512]{2,1,0:T(4,128)(2,1)}), bf16[32,4,512]{2,1,0:T(4,128)(2,1)S(1)}, u32[]{:S(2)}, u32[]{:S(2)}) async-start(bf16[32,4,512]{2,1,0:T(4,128)(2,1)} %reshape.518), calls=%async_computation | async-start | bytes 262144 | tf_op jit(solution)/shard_map/all_to_all | solution.py:83
  14.4 16.8 %copy-start.41 = (f32[1536]{0:T(1024)}, f32[1536]{0:T(1024)S(1)}, u32[]{:S(2)}) copy-start(f32[1536]{0:T(1024)S(1)} %fusion.133) | copy-start | bytes 18436
  15.1 16.1 %copy-start.67 = (s32[1536]{0:T(1024)}, s32[1536]{0:T(1024)S(1)}, u32[]{:S(2)}) copy-start(s32[1536]{0:T(1024)S(1)} %reduce.1) | copy-start | bytes 18436
  16.6 28.1 %copy-start.48 = (f32[1,512]{1,0:T(1,128)}, f32[1,512]{1,0:T(1,128)S(1)}, u32[]{:S(2)}) copy-start(f32[1,512]{1,0:T(1,128)S(1)} %get-tuple-element.27) | copy-start | bytes 6148
  16.6 64.8 %copy-start.50 = (f32[1,512]{1,0:T(1,128)}, f32[1,512]{1,0:T(1,128)S(1)}, u32[]{:S(2)}) copy-start(f32[1,512]{1,0:T(1,128)S(1)} %get-tuple-element.26) | copy-start | bytes 6148
  43.0 18.7 %copy-start.26 = (f32[128,512]{1,0:T(8,128)}, f32[128,512]{1,0:T(8,128)S(1)}, u32[]{:S(2)}) copy-start(f32[128,512]{1,0:T(8,128)S(1)} %scatter_custom_fusion) | copy-start | bytes 786436
  45.4 36.0 %copy-start.33 = (bf16[128,512]{1,0:T(8,128)(2,1)}, bf16[128,512]{1,0:T(8,128)(2,1)S(1)}, u32[]{:S(2)}) copy-start(bf16[128,512]{1,0:T(8,128)(2,1)S(1)} %add_convert_fusion.3) | copy-start | bytes 393220
  48.3 14.0 %all-to-all-start.1 = ((bf16[32,4,512]{2,1,0:T(4,128)(2,1)}), bf16[32,4,512]{2,1,0:T(4,128)(2,1)S(1)}, u32[]{:S(2)}, u32[]{:S(2)}) async-start(bf16[32,4,512]{2,1,0:T(4,128)(2,1)} %reshape.542), calls=%async_computation.1 | async-start | bytes 262144 | tf_op jit(solution)/shard_map/all_to_all | solution.py:83
  54.7 49.1 %copy-start.68 = (s32[1536]{0:T(1024)}, s32[1536]{0:T(1024)S(1)}, u32[]{:S(2)}) copy-start(s32[1536]{0:T(1024)S(1)} %reduce.4) | copy-start | bytes 18436
  79.7 17.8 %copy-start.28 = (f32[128,512]{1,0:T(8,128)}, f32[128,512]{1,0:T(8,128)S(1)}, u32[]{:S(2)}) copy-start(f32[128,512]{1,0:T(8,128)S(1)} %scatter_custom_fusion.1) | copy-start | bytes 786436
  81.1 16.3 %copy-start.71 = (f32[128]{0:T(128)}, f32[128]{0:T(128)S(1)}, u32[]{:S(2)}) copy-start(f32[128]{0:T(128)S(1)} %broadcast_multiply_fusion.10) | copy-start | bytes 1540
  82.1 35.1 %copy-start.35 = (bf16[128,512]{1,0:T(8,128)(2,1)}, bf16[128,512]{1,0:T(8,128)(2,1)S(1)}, u32[]{:S(2)}) copy-start(bf16[128,512]{1,0:T(8,128)(2,1)S(1)} %add_convert_fusion.2) | copy-start | bytes 393220
  85.0 13.4 %all-to-all-start.2 = ((bf16[32,4,512]{2,1,0:T(4,128)(2,1)}), bf16[32,4,512]{2,1,0:T(4,128)(2,1)S(1)}, u32[]{:S(2)}, u32[]{:S(2)}) async-start(bf16[32,4,512]{2,1,0:T(4,128)(2,1)} %reshape.566), calls=%async_computation.2 | async-start | bytes 262144 | tf_op jit(solution)/shard_map/all_to_all | solution.py:83
  115.5 20.7 %copy-start.30 = (f32[128,512]{1,0:T(8,128)}, f32[128,512]{1,0:T(8,128)S(1)}, u32[]{:S(2)}) copy-start(f32[128,512]{1,0:T(8,128)S(1)} %scatter_custom_fusion.2) | copy-start | bytes 786436
  121.4 20.8 %all-to-all-start.3 = ((bf16[32,4,512]{2,1,0:T(4,128)(2,1)}), bf16[32,4,512]{2,1,0:T(4,128)(2,1)S(1)}, u32[]{:S(2)}, u32[]{:S(2)}) async-start(bf16[32,4,512]{2,1,0:T(4,128)(2,1)} %reshape.590), calls=%async_computation.3 | async-start | bytes 262144 | tf_op jit(solution)/shard_map/all_to_all | solution.py:83
  172.2 23.3 %copy-start.6 = (f32[512,512]{1,0:T(8,128)S(1)}, f32[512,512]{1,0:T(8,128)}, u32[]{:S(2)}) copy-start(f32[512,512]{1,0:T(8,128)} %scatter_custom_fusion.3) | copy-start | bytes 3145732
  177.0 33.6 %copy-start.12 = (bf16[512,512]{1,0:T(8,128)(2,1)S(1)}, bf16[512,512]{1,0:T(8,128)(2,1)}, u32[]{:S(2)}) copy-start(bf16[512,512]{1,0:T(8,128)(2,1)} %param.17) | copy-start | bytes 1572868
  189.7 22.5 %all-to-all-start.4 = ((bf16[32,4,512]{2,1,0:T(4,128)(2,1)}), bf16[32,4,512]{2,1,0:T(4,128)(2,1)S(1)}, u32[]{:S(2)}, u32[]{:S(2)}) async-start(bf16[32,4,512]{2,1,0:T(4,128)(2,1)} %reshape.509), calls=%async_computation.4 | async-start | bytes 262144 | tf_op jit(solution)/shard_map/all_to_all | solution.py:83
  225.8 31.9 %copy-start.36 = (bf16[128,512]{1,0:T(8,128)(2,1)S(1)}, bf16[128,512]{1,0:T(8,128)(2,1)}, u32[]{:S(2)}) copy-start(bf16[128,512]{1,0:T(8,128)(2,1)} %copy-done.35) | copy-start | bytes 393220
  230.3 28.7 %copy-start.19 = (f32[1,512,512]{1,2,0:T(8,128)S(1)}, f32[1,512,512]{1,2,0:T(8,128)}, u32[]{:S(2)}) copy-start(f32[1,512,512]{1,2,0:T(8,128)} %convolution_bitcast_fusion) | copy-start | bytes 3145732
  251.7 14.1 %all-to-all-start.5 = ((bf16[32,4,512]{2,1,0:T(4,128)(2,1)}), bf16[32,4,512]{2,1,0:T(4,128)(2,1)}, u32[]{:S(2)}, u32[]{:S(2)}) async-start(bf16[32,4,512]{2,1,0:T(4,128)(2,1)} %reshape.510), calls=%async_computation.5 | async-start | bytes 262144 | tf_op jit(solution)/shard_map/all_to_all | solution.py:83
  279.9 30.0 %copy-start.34 = (bf16[128,512]{1,0:T(8,128)(2,1)S(1)}, bf16[128,512]{1,0:T(8,128)(2,1)}, u32[]{:S(2)}) copy-start(bf16[128,512]{1,0:T(8,128)(2,1)} %copy-done.33) | copy-start | bytes 393220
  284.4 26.8 %copy-start.17 = (f32[1,512,512]{1,2,0:T(8,128)S(1)}, f32[1,512,512]{1,2,0:T(8,128)}, u32[]{:S(2)}) copy-start(f32[1,512,512]{1,2,0:T(8,128)} %convolution_bitcast_fusion.3) | copy-start | bytes 3145732
  305.9 12.2 %all-to-all-start.6 = ((bf16[32,4,512]{2,1,0:T(4,128)(2,1)}), bf16[32,4,512]{2,1,0:T(4,128)(2,1)}, u32[]{:S(2)}, u32[]{:S(2)}) async-start(bf16[32,4,512]{2,1,0:T(4,128)(2,1)} %reshape.511), calls=%async_computation.6 | async-start | bytes 262144 | tf_op jit(solution)/shard_map/all_to_all | solution.py:83
  332.0 29.8 %copy-start.38 = (bf16[128,512]{1,0:T(8,128)(2,1)S(1)}, bf16[128,512]{1,0:T(8,128)(2,1)}, u32[]{:S(2)}) copy-start(bf16[128,512]{1,0:T(8,128)(2,1)} %param.18) | copy-start | bytes 393220
  332.0 31.2 %copy-start.61 = (f32[512]{0:T(512)S(1)}, f32[512]{0:T(512)}, u32[]{:S(2)}) copy-start(f32[512]{0:T(512)} %get-tuple-element.9) | copy-start | bytes 6148
  332.0 31.1 %copy-start.62 = (f32[512]{0:T(512)S(1)}, f32[512]{0:T(512)}, u32[]{:S(2)}) copy-start(f32[512]{0:T(512)} %get-tuple-element.16) | copy-start | bytes 6148
  336.4 27.4 %copy-start.16 = (f32[1,512,512]{1,2,0:T(8,128)S(1)}, f32[1,512,512]{1,2,0:T(8,128)}, u32[]{:S(2)}) copy-start(f32[1,512,512]{1,2,0:T(8,128)} %convolution_bitcast_fusion.6) | copy-start | bytes 3145732
  336.4 27.5 %copy-start.18 = (f32[1,512,512]{1,2,0:T(8,128)S(1)}, f32[1,512,512]{1,2,0:T(8,128)}, u32[]{:S(2)}) copy-start(f32[1,512,512]{1,2,0:T(8,128)} %convolution_bitcast_fusion.7) | copy-start | bytes 3145732
  357.9 12.1 %all-to-all-start.7 = ((bf16[32,4,512]{2,1,0:T(4,128)(2,1)}), bf16[32,4,512]{2,1,0:T(4,128)(2,1)S(1)}, u32[]{:S(2)}, u32[]{:S(2)}) async-start(bf16[32,4,512]{2,1,0:T(4,128)(2,1)} %reshape.512), calls=%async_computation.7 | async-start | bytes 262144 | tf_op jit(solution)/shard_map/all_to_all | solution.py:83
  (54 other events, 376.4 us)
where the time goes:
time: 613 us; the launch traced here: 602 us
  blocking collectives  211 us (34%)
  other arithmetic  192 us (31%)
  local copies, waits for them, and re-layouts  95.8 us (16%)
  matrix products  48.4 us (8%)
  starting transfers between devices  43.1 us (7%)
  waiting for transfers between devices  8.05 us (1%)
    psum x1, blocking collectives, shards(): lax.psum((weight_stack, gain_stack), ('lat', 'lon'))  211 us
    scatter-add x4, other arithmetic, edge_forward(): jax.ops.segment_sum(hidden, receivers, num_segments=proj_recv.shape[0])  48.4 us
    all_to_all x8, starting transfers between devices, trade(): lax.all_to_all(buffer, ('lat', 'lon'), split_axis=0, concat_axis=0, tiled...  43.1 us
    scatter-add x4, other arithmetic, edge_backward(): jax.ops.segment_sum(grad_pre, senders, num_segments=slot_count)  41.9 us
    scatter-add x4, other arithmetic, edge_backward(): jax.ops.segment_sum(grad_pre, receivers, num_segments=recv_count)  41.7 us
    gather x4, local copies, waits for them, and re-layouts, edge_forward(): slot_vals[senders].astype(jnp.float32)  22 us
    gather x4, local copies, waits for them, and re-layouts, edge_forward(): proj_recv[receivers].astype(jnp.float32)  21.1 us
    unnamed x163, local copies, waits for them, and re-layouts  20.5 us
  transfers between devices with their start and end apart: 8, of which 5 were waited for; matrix products, arithmetic and copies ran while one was open for 13% of the time, Pallas kernels for 0%

commit v1 on v0

--- a/solution.py
+++ b/solution.py
@@ -215,7 +215,8 @@
     weight_parts[0], gain_parts[0] = settle(grad_weights, gain_part)
     weight_stack = jnp.stack(weight_parts)
     gain_stack = jnp.stack(gain_parts)
-    weight_stack, gain_stack = lax.psum((weight_stack, gain_stack), ("lat", "lon"))
+    pass_face = lambda shard_in: lax.psum(lax.psum(shard_in, "lon"), "lat")
+    weight_stack, gain_stack = pass_face((weight_stack, gain_stack))
     return (grid_out, weight_stack.astype(jnp.bfloat16), gain_stack)
 
 

time: 613 us -> 1010 us (1.65)
  blocking collectives: 211 us -> 439 us
  waiting for transfers between devices: 8.05 us -> 164 us
  between operations: 4.38 us -> 17.7 us
    psum x1 -> x2, blocking collectives: 211 us -> 439 us  [shards(): pass_face = lambda shard_in: lax.psum(lax.psum(shard_in, 'lon'), 'lat')]
    psum x0 -> x1, waiting for transfers between devices: none -> 155 us  [shards(): pass_face = lambda shard_in: lax.psum(lax.psum(shard_in, 'lon'), 'lat')]
    unnamed x163 -> x169, local copies, waits for them, and re-layouts: 20.5 us -> 20.5 us
  transfers between devices with their start and end apart: 8 -> 9, of which waited for: 5 -> 6; matrix products, arithmetic and copies ran while one was open for 13% -> 7% of each run, Pallas kernels for 0% -> 0%
where the time goes in v1:
time: 1010 us; the launch traced here: 999 us
  blocking collectives  439 us (43%)
  other arithmetic  191 us (19%)
  waiting for transfers between devices  164 us (16%)
  local copies, waits for them, and re-layouts  95.7 us (9%)
  matrix products  48.4 us (5%)
  starting transfers between devices  43.1 us (4%)
  between operations  17.7 us (2%)
    psum x2, blocking collectives, shards(): pass_face = lambda shard_in: lax.psum(lax.psum(shard_in, 'lon'), 'lat')  439 us
    psum x1, waiting for transfers between devices, shards(): pass_face = lambda shard_in: lax.psum(lax.psum(shard_in, 'lon'), 'lat')  155 us
    scatter-add x4, other arithmetic, edge_forward(): jax.ops.segment_sum(hidden, receivers, num_segments=proj_recv.shape[0])  48.4 us
    all_to_all x8, starting transfers between devices, trade(): lax.all_to_all(buffer, ('lat', 'lon'), split_axis=0, concat_axis=0, tiled...  43.1 us
    scatter-add x4, other arithmetic, edge_backward(): jax.ops.segment_sum(grad_pre, senders, num_segments=slot_count)  41.9 us
    scatter-add x4, other arithmetic, edge_backward(): jax.ops.segment_sum(grad_pre, receivers, num_segments=recv_count)  41.7 us
    gather x4, local copies, waits for them, and re-layouts, edge_forward(): slot_vals[senders].astype(jnp.float32)  22 us
    gather x4, local copies, waits for them, and re-layouts, edge_forward(): proj_recv[receivers].astype(jnp.float32)  21.1 us
  transfers between devices with their start and end apart: 9, of which 6 were waited for; matrix products, arithmetic and copies ran while one was open for 7% of the time, Pallas kernels for 0%

profile of v1, /device:TPU:0, one launch (start us, length us, event | category | flops | bytes accessed | tf_op | source)
XLA Modules:
  0.0 999.0 jit_solution(6283096260542524367)
XLA Ops:
  11.4 7.3 all-to-all-start
  32.3 5.4 gather_fusion.1
  37.7 11.8 %scatter_custom_fusion = f32[128,512]{1,0:T(8,128)S(1)} fusion(s32[1536]{0:T(1024)S(1)} %reduce.1, bf16[1536,512]{1,0:T(8,128)(2,1)S(1)} %gather_fusion.2, bf16[1536,512]{1,0:T(8,128)(2,1)} %gather_fusion.1, f32[1536]{0:T(1024)S(1)} %fusion.133, f32[]{:T(128)} %constant.63.clone.1, f32[]{:T(128)} %constant.59.clone.1), kind=kCustom, calls=%fused_computation.56 | custom fusion | flops 7077888 | bytes 3416072 | tf_op jit(solution)/shard_map/scatter-add | solution.py:37
  54.8 5.8 all-to-all-start.1
  62.7 5.4 gather_fusion.5
  68.9 5.4 gather_fusion.4
  74.3 11.9 %scatter_custom_fusion.1 = f32[128,512]{1,0:T(8,128)S(1)} fusion(s32[1536]{0:T(1024)S(1)} %reduce.4, bf16[1536,512]{1,0:T(8,128)(2,1)} %gather_fusion.5, bf16[1536,512]{1,0:T(8,128)(2,1)} %gather_fusion.4, f32[1536]{0:T(1024)S(1)} %fusion.134, f32[]{:T(128)} %constant.63.clone.1, f32[]{:T(128)} %constant.59.clone.1), kind=kCustom, calls=%fused_computation.51 | custom fusion | flops 7077888 | bytes 3416072 | tf_op jit(solution)/shard_map/scatter-add | solution.py:37
  91.5 5.2 all-to-all-start.2
  98.5 5.4 gather_fusion.8
  104.9 5.4 gather_fusion.7
  110.3 11.7 %scatter_custom_fusion.2 = f32[128,512]{1,0:T(8,128)S(1)} fusion(s32[1536]{0:T(1024)S(1)} %reduce.4, bf16[1536,512]{1,0:T(8,128)(2,1)} %gather_fusion.8, bf16[1536,512]{1,0:T(8,128)(2,1)} %gather_fusion.7, f32[1536]{0:T(1024)S(1)} %fusion.134, f32[]{:T(128)} %constant.63.clone.1, f32[]{:T(128)} %constant.59.clone.1), kind=kCustom, calls=%fused_computation.46 | custom fusion | flops 7077888 | bytes 3416072 | tf_op jit(solution)/shard_map/scatter-add | solution.py:37
  127.9 4.9 all-to-all-start.3
  142.7 5.4 gather_fusion.11
  148.8 5.7 gather_fusion.10
  154.5 13.0 %scatter_custom_fusion.3 = f32[512,512]{1,0:T(8,128)} fusion(s32[1536]{0:T(1024)} %reduce, bf16[1536,512]{1,0:T(8,128)(2,1)S(1)} %copy-done.3, bf16[1536,512]{1,0:T(8,128)(2,1)} %gather_fusion.10, f32[1536]{0:T(1024)} %fusion.135, f32[]{:T(128)} %constant.63.clone.1, f32[]{:T(128)} %constant.59.clone.1), kind=kCustom, calls=%fused_computation.41 | custom fusion | flops 7077888 | bytes 4203520 | tf_op jit(solution)/shard_map/scatter-add | solution.py:37
  183.5 11.0 %scatter_custom_fusion.4 = f32[128,512]{1,0:T(8,128)} fusion(s32[1536]{0:T(1024)} %reduce.10, f32[1536,512]{1,0:T(8,128)} %multiply_multiply_fusion.3, f32[]{:T(128)} %constant.59.clone.1), kind=kCustom, calls=%fused_computation.206 | custom fusion | flops 786432 | bytes 262656 | tf_op jit(solution)/shard_map/scatter-add | solution.py:76
  196.1 5.8 all-to-all-start.4
  204.6 10.5 %scatter_custom_fusion.15 = f32[512,512]{1,0:T(8,128)S(1)} fusion(s32[1536]{0:T(1024)} %reduce, f32[1536,512]{1,0:T(8,128)} %multiply_multiply_fusion.3, f32[]{:T(128)} %constant.59.clone.1), kind=kCustom, calls=%fused_computation.141 | custom fusion | flops 786432 | bytes 1049088 | tf_op jit(solution)/shard_map/scatter-add | solution.py:73
  234.8 10.4 %scatter_custom_fusion.6 = f32[128,512]{1,0:T(8,128)S(1)} fusion(s32[1536]{0:T(1024)} %copy-done.71, f32[1536,512]{1,0:T(8,128)} %multiply_multiply_fusion.2, f32[]{:T(128)} %constant.59.clone.1), kind=kCustom, calls=%fused_computation.202 | custom fusion | flops 786432 | bytes 262656 | tf_op jit(solution)/shard_map/scatter-add | solution.py:73
  245.2 10.3 %scatter_custom_fusion.7 = f32[128,512]{1,0:T(8,128)S(1)} fusion(s32[1536]{0:T(1024)} %reduce.11, f32[1536,512]{1,0:T(8,128)} %multiply_multiply_fusion.2, f32[]{:T(128)} %constant.59.clone.1), kind=kCustom, calls=%fused_computation.200 | custom fusion | flops 786432 | bytes 262656 | tf_op jit(solution)/shard_map/scatter-add | solution.py:76
  256.2 6.0 all-to-all-start.5
  279.4 4.9 gather_fusion.14
  288.9 10.4 %scatter_custom_fusion.9 = f32[128,512]{1,0:T(8,128)S(1)} fusion(s32[1536]{0:T(1024)} %copy-done.71, f32[1536,512]{1,0:T(8,128)} %multiply_multiply_fusion.1, f32[]{:T(128)} %constant.59.clone.1), kind=kCustom, calls=%fused_computation.196 | custom fusion | flops 786432 | bytes 262656 | tf_op jit(solution)/shard_map/scatter-add | solution.py:73
  299.3 10.3 %scatter_custom_fusion.10 = f32[128,512]{1,0:T(8,128)S(1)} fusion(s32[1536]{0:T(1024)} %reduce.11, f32[1536,512]{1,0:T(8,128)} %multiply_multiply_fusion.1, f32[]{:T(128)} %constant.59.clone.1), kind=kCustom, calls=%fused_computation.194 | custom fusion | flops 786432 | bytes 262656 | tf_op jit(solution)/shard_map/scatter-add | solution.py:76
  331.6 4.9 gather_fusion.15
  340.9 10.5 %scatter_custom_fusion.14 = f32[128,512]{1,0:T(8,128)S(1)} fusion(s32[1536]{0:T(1024)} %copy-done.70, f32[1536,512]{1,0:T(8,128)} %multiply_multiply_fusion, f32[]{:T(128)} %constant.59.clone.1), kind=kCustom, calls=%fused_computation.188 | custom fusion | flops 786432 | bytes 262656 | tf_op jit(solution)/shard_map/scatter-add | solution.py:73
  351.4 10.3 %scatter_custom_fusion.12 = f32[128,512]{1,0:T(8,128)S(1)} fusion(s32[1536]{0:T(1024)} %reduce.9, f32[1536,512]{1,0:T(8,128)} %multiply_multiply_fusion, f32[]{:T(128)} %constant.59.clone.1), kind=kCustom, calls=%fused_computation.190 | custom fusion | flops 786432 | bytes 262656 | tf_op jit(solution)/shard_map/scatter-add | solution.py:76
  380.4 6.7 pad_maximum_fusion
  389.2 13.5 %psum.30 = f32[4,512]{1,0:T(4,128)S(1)} all-reduce(f32[4,512]{1,0:T(4,128)S(1)} %pad_maximum_fusion.1), channel_id=1, replica_groups=mesh['lat'=4,'lon'=8] {'lon'}, use_global_device_ids=true, to_apply=%region_38.39 | all-reduce | flops 2048 | bytes 16384 | tf_op jit(solution)/shard_map/psum | solution.py:218
  402.7 154.9 %all-reduce.4.cloned.1.call-done = f32[4,3,512,512]{2,3,1,0:T(8,128)} async-done(((f32[4,3,512,512]{2,3,1,0:T(8,128)}), f32[4,3,512,512]{2,3,1,0:T(8,128)}) %all-reduce.4.cloned.1.call-update) | async-done | bytes 12582928 | tf_op jit(solution)/shard_map/psum | solution.py:218
  557.6 425.6 %all-reduce.5 = (bf16[4,3,512,512]{2,3,1,0:T(8,128)(2,1)}, f32[4,512]{1,0:T(4,128)}) all-reduce(f32[4,3,512,512]{2,3,1,0:T(8,128)} %all-reduce.4.cloned.1.call-done, f32[4,512]{1,0:T(4,128)S(1)} %psum.30), channel_id=1, replica_groups=mesh['lat'=4,'lon'=8] {'lat'}, use_global_device_ids=true, to_apply=%region_33.34 | all-reduce | flops 3147776 | bytes 18890752 | tf_op jit(solution)/shard_map/psum | solution.py:218
  983.1 8.6 copy.57
  (320 shorter events, 156.8 us)
Async XLA Ops:
  7.3 15.2 %copy-start.69 = (f32[4,512]{1,0:T(4,128)S(1)}, f32[4,512]{1,0:T(4,128)}, u32[]{:S(2)}) copy-start(f32[4,512]{1,0:T(4,128)} %param.20) | copy-start | bytes 24580
  7.3 17.3 %copy-start.38 = (bf16[128,512]{1,0:T(8,128)(2,1)S(1)}, bf16[128,512]{1,0:T(8,128)(2,1)}, u32[]{:S(2)}) copy-start(bf16[128,512]{1,0:T(8,128)(2,1)} %param.18) | copy-start | bytes 393220
  11.4 20.8 %all-to-all-start = ((bf16[32,4,512]{2,1,0:T(4,128)(2,1)}), bf16[32,4,512]{2,1,0:T(4,128)(2,1)S(1)}, u32[]{:S(2)}, u32[]{:S(2)}) async-start(bf16[32,4,512]{2,1,0:T(4,128)(2,1)} %reshape.518), calls=%async_computation | async-start | bytes 262144 | tf_op jit(solution)/shard_map/all_to_all | solution.py:83
  20.9 16.7 %copy-start.42 = (f32[1536]{0:T(1024)}, f32[1536]{0:T(1024)S(1)}, u32[]{:S(2)}) copy-start(f32[1536]{0:T(1024)S(1)} %fusion.133) | copy-start | bytes 18436
  21.6 16.1 %copy-start.70 = (s32[1536]{0:T(1024)}, s32[1536]{0:T(1024)S(1)}, u32[]{:S(2)}) copy-start(s32[1536]{0:T(1024)S(1)} %reduce.1) | copy-start | bytes 18436
  23.1 28.1 %copy-start.49 = (f32[1,512]{1,0:T(1,128)}, f32[1,512]{1,0:T(1,128)S(1)}, u32[]{:S(2)}) copy-start(f32[1,512]{1,0:T(1,128)S(1)} %get-tuple-element.27) | copy-start | bytes 6148
  23.1 64.8 %copy-start.51 = (f32[1,512]{1,0:T(1,128)}, f32[1,512]{1,0:T(1,128)S(1)}, u32[]{:S(2)}) copy-start(f32[1,512]{1,0:T(1,128)S(1)} %get-tuple-element.26) | copy-start | bytes 6148
  49.5 18.7 %copy-start.26 = (f32[128,512]{1,0:T(8,128)}, f32[128,512]{1,0:T(8,128)S(1)}, u32[]{:S(2)}) copy-start(f32[128,512]{1,0:T(8,128)S(1)} %scatter_custom_fusion) | copy-start | bytes 786436
  51.9 36.0 %copy-start.34 = (bf16[128,512]{1,0:T(8,128)(2,1)}, bf16[128,512]{1,0:T(8,128)(2,1)S(1)}, u32[]{:S(2)}) copy-start(bf16[128,512]{1,0:T(8,128)(2,1)S(1)} %add_convert_fusion.3) | copy-start | bytes 393220
  54.8 14.0 %all-to-all-start.1 = ((bf16[32,4,512]{2,1,0:T(4,128)(2,1)}), bf16[32,4,512]{2,1,0:T(4,128)(2,1)S(1)}, u32[]{:S(2)}, u32[]{:S(2)}) async-start(bf16[32,4,512]{2,1,0:T(4,128)(2,1)} %reshape.542), calls=%async_computation.1 | async-start | bytes 262144 | tf_op jit(solution)/shard_map/all_to_all | solution.py:83
  61.2 49.1 %copy-start.71 = (s32[1536]{0:T(1024)}, s32[1536]{0:T(1024)S(1)}, u32[]{:S(2)}) copy-start(s32[1536]{0:T(1024)S(1)} %reduce.4) | copy-start | bytes 18436
  86.2 17.8 %copy-start.28 = (f32[128,512]{1,0:T(8,128)}, f32[128,512]{1,0:T(8,128)S(1)}, u32[]{:S(2)}) copy-start(f32[128,512]{1,0:T(8,128)S(1)} %scatter_custom_fusion.1) | copy-start | bytes 786436
  87.6 16.3 %copy-start.74 = (f32[128]{0:T(128)}, f32[128]{0:T(128)S(1)}, u32[]{:S(2)}) copy-start(f32[128]{0:T(128)S(1)} %broadcast_multiply_fusion.10) | copy-start | bytes 1540
  88.6 35.1 %copy-start.36 = (bf16[128,512]{1,0:T(8,128)(2,1)}, bf16[128,512]{1,0:T(8,128)(2,1)S(1)}, u32[]{:S(2)}) copy-start(bf16[128,512]{1,0:T(8,128)(2,1)S(1)} %add_convert_fusion.2) | copy-start | bytes 393220
  91.5 13.4 %all-to-all-start.2 = ((bf16[32,4,512]{2,1,0:T(4,128)(2,1)}), bf16[32,4,512]{2,1,0:T(4,128)(2,1)S(1)}, u32[]{:S(2)}, u32[]{:S(2)}) async-start(bf16[32,4,512]{2,1,0:T(4,128)(2,1)} %reshape.566), calls=%async_computation.2 | async-start | bytes 262144 | tf_op jit(solution)/shard_map/all_to_all | solution.py:83
  122.0 20.7 %copy-start.30 = (f32[128,512]{1,0:T(8,128)}, f32[128,512]{1,0:T(8,128)S(1)}, u32[]{:S(2)}) copy-start(f32[128,512]{1,0:T(8,128)S(1)} %scatter_custom_fusion.2) | copy-start | bytes 786436
  127.9 20.8 %all-to-all-start.3 = ((bf16[32,4,512]{2,1,0:T(4,128)(2,1)}), bf16[32,4,512]{2,1,0:T(4,128)(2,1)S(1)}, u32[]{:S(2)}, u32[]{:S(2)}) async-start(bf16[32,4,512]{2,1,0:T(4,128)(2,1)} %reshape.590), calls=%async_computation.3 | async-start | bytes 262144 | tf_op jit(solution)/shard_map/all_to_all | solution.py:83
  154.5 15.2 %copy-start.60 = (f32[1,512]{1,0:T(1,128)S(1)}, f32[1,512]{1,0:T(1,128)}, u32[]{:S(2)}) copy-start(f32[1,512]{1,0:T(1,128)} %get-tuple-element.25) | copy-start | bytes 6148
  178.7 23.3 %copy-start.6 = (f32[512,512]{1,0:T(8,128)S(1)}, f32[512,512]{1,0:T(8,128)}, u32[]{:S(2)}) copy-start(f32[512,512]{1,0:T(8,128)} %scatter_custom_fusion.3) | copy-start | bytes 3145732
  183.5 31.5 %copy-start.12 = (bf16[512,512]{1,0:T(8,128)(2,1)S(1)}, bf16[512,512]{1,0:T(8,128)(2,1)}, u32[]{:S(2)}) copy-start(bf16[512,512]{1,0:T(8,128)(2,1)} %param.17) | copy-start | bytes 1572868
  196.1 20.4 %all-to-all-start.4 = ((bf16[32,4,512]{2,1,0:T(4,128)(2,1)}), bf16[32,4,512]{2,1,0:T(4,128)(2,1)S(1)}, u32[]{:S(2)}, u32[]{:S(2)}) async-start(bf16[32,4,512]{2,1,0:T(4,128)(2,1)} %reshape.509), calls=%async_computation.4 | async-start | bytes 262144 | tf_op jit(solution)/shard_map/all_to_all | solution.py:83
  230.2 31.9 %copy-start.37 = (bf16[128,512]{1,0:T(8,128)(2,1)S(1)}, bf16[128,512]{1,0:T(8,128)(2,1)}, u32[]{:S(2)}) copy-start(bf16[128,512]{1,0:T(8,128)(2,1)} %copy-done.36) | copy-start | bytes 393220
  234.8 28.8 %copy-start.19 = (f32[1,512,512]{1,2,0:T(8,128)S(1)}, f32[1,512,512]{1,2,0:T(8,128)}, u32[]{:S(2)}) copy-start(f32[1,512,512]{1,2,0:T(8,128)} %convolution_bitcast_fusion) | copy-start | bytes 3145732
  256.2 14.1 %all-to-all-start.5 = ((bf16[32,4,512]{2,1,0:T(4,128)(2,1)}), bf16[32,4,512]{2,1,0:T(4,128)(2,1)}, u32[]{:S(2)}, u32[]{:S(2)}) async-start(bf16[32,4,512]{2,1,0:T(4,128)(2,1)} %reshape.510), calls=%async_computation.5 | async-start | bytes 262144 | tf_op jit(solution)/shard_map/all_to_all | solution.py:83
  284.3 30.1 %copy-start.35 = (bf16[128,512]{1,0:T(8,128)(2,1)S(1)}, bf16[128,512]{1,0:T(8,128)(2,1)}, u32[]{:S(2)}) copy-start(bf16[128,512]{1,0:T(8,128)(2,1)} %copy-done.34) | copy-start | bytes 393220
  288.9 26.8 %copy-start.17 = (f32[1,512,512]{1,2,0:T(8,128)S(1)}, f32[1,512,512]{1,2,0:T(8,128)}, u32[]{:S(2)}) copy-start(f32[1,512,512]{1,2,0:T(8,128)} %convolution_bitcast_fusion.3) | copy-start | bytes 3145732
  310.3 12.3 %all-to-all-start.6 = ((bf16[32,4,512]{2,1,0:T(4,128)(2,1)}), bf16[32,4,512]{2,1,0:T(4,128)(2,1)}, u32[]{:S(2)}, u32[]{:S(2)}) async-start(bf16[32,4,512]{2,1,0:T(4,128)(2,1)} %reshape.511), calls=%async_computation.6 | async-start | bytes 262144 | tf_op jit(solution)/shard_map/all_to_all | solution.py:83
  336.5 29.8 %copy-start.39 = (bf16[128,512]{1,0:T(8,128)(2,1)S(1)}, bf16[128,512]{1,0:T(8,128)(2,1)}, u32[]{:S(2)}) copy-start(bf16[128,512]{1,0:T(8,128)(2,1)} %param.18) | copy-start | bytes 393220
  340.9 26.8 %copy-start.16 = (f32[1,512,512]{1,2,0:T(8,128)S(1)}, f32[1,512,512]{1,2,0:T(8,128)}, u32[]{:S(2)}) copy-start(f32[1,512,512]{1,2,0:T(8,128)} %convolution_bitcast_fusion.6) | copy-start | bytes 3145732
  340.9 26.8 %copy-start.18 = (f32[1,512,512]{1,2,0:T(8,128)S(1)}, f32[1,512,512]{1,2,0:T(8,128)}, u32[]{:S(2)}) copy-start(f32[1,512,512]{1,2,0:T(8,128)} %convolution_bitcast_fusion.7) | copy-start | bytes 3145732
  362.4 12.1 %all-to-all-start.7 = ((bf16[32,4,512]{2,1,0:T(4,128)(2,1)}), bf16[32,4,512]{2,1,0:T(4,128)(2,1)S(1)}, u32[]{:S(2)}, u32[]{:S(2)}) async-start(bf16[32,4,512]{2,1,0:T(4,128)(2,1)} %reshape.512), calls=%async_computation.7 | async-start | bytes 262144 | tf_op jit(solution)/shard_map/all_to_all | solution.py:83
  366.3 191.3 %all-reduce.4.cloned.1.call-start = ((), (), s32[]{:S(2)}) async-start(), calls=%async_computation.8 | async-start | bytes 25165824 | tf_op jit(solution)/shard_map/psum | solution.py:218
  (58 other events, 371.9 us)
Sparse Core Ops, SparseCore 0:
  387.2 170.2 all-reduce.3
